TPU v7x, 32 devices: a whole 2x2x4 slice. The times are simulated.
32 devices in a mesh: gx: 4 (over x, core), gy: 4 (over z), gz: 2 (over y).
Axes of the slice: x: 2, y: 2, z: 4, core: 2. Of those that a mesh axis runs over, the one named last changes fastest.
Arguments:
- occupied: float32 [16, 16, 16, 256], P(None, 'gx', 'gy', 'gz'), may hold values from -6 to 6
- virtual: float32 [16, 16, 16, 256], P(None, 'gx', 'gy', 'gz'), may hold values from -6 to 6
- kernel_fields: float32 [4, 16, 16, 256], P(None, 'gx', 'gy', 'gz'), may hold values from -1.5 to 1.5
- density_grad: float32 [3, 16, 16, 256], P(None, 'gx', 'gy', 'gz'), may hold values from -6 to 6
Outputs:
- potential: float32 [256, 16, 16, 256], P(None, 'gx', 'gy', 'gz')
- casida: float32 [256, 256], P(('gx', 'gy', 'gz'))
All inputs are finite; a program needn't handle non-finite values.
Results may differ from a plain program's by a relative error of at most 0.00013.
Values sent between devices are 32-bit elements; how exact they have to be, the bound alone decides.
No kernel may reach another device: no remote copies, remote signals or barrier semaphores. Data moves between devices by JAX's collectives and lax.ppermute only.
A program may use at most 64 MiB of HBM per device.

v0:
```python
import jax
import jax.numpy as jnp
from jax import lax
from jax.sharding import PartitionSpec as P


def padded(block, sides, width):
    for axis, dim in sides:
        count = lax.axis_size(axis)
        forward = [(i, i + 1) for i in range(count - 1)]
        forward.append((count - 1, 0))
        backward = [(target, source) for source, target in forward]
        low = lax.ppermute(
            lax.slice_in_dim(block, block.shape[dim] - width, None, axis=dim), axis, forward
        )
        high = lax.ppermute(lax.slice_in_dim(block, 0, width, axis=dim), axis, backward)
        block = jnp.concatenate([low, block, high], axis=dim)
    return block


def window(values, offsets):
    starts = (0,) + tuple((2 + offsets[dimension] for dimension in range(3)))
    limits = (values.shape[0],) + tuple(
        (values.shape[dimension + 1] - 2 + offsets[dimension] for dimension in range(3))
    )
    return lax.slice(values, starts, limits)


def derivative(values, dimension):

    def shifted(offset):
        offsets = [0, 0, 0]
        offsets[dimension] = offset
        return window(values, offsets)

    inner_diff = shifted(1) - shifted(-1)
    outer_diff = shifted(2) - shifted(-2)
    return (8.0 * inner_diff - outer_diff) / 12.0


def trim_rim(values, margin):
    return values[:, margin:-margin, margin:-margin, margin:-margin]


def on_device(occupied, virtual, kernel_fields, density_grad):
    local_kernel = kernel_fields[0]
    mixed_kernel = kernel_fields[1]
    nvir = virtual.shape[0]
    occ_wide = padded(occupied, (("gx", 1), ("gy", 2), ("gz", 3)), 4)
    vir_wide = padded(virtual, (("gx", 1), ("gy", 2), ("gz", 3)), 4)
    stacked = jnp.concatenate([kernel_fields, density_grad], axis=0)
    field_wide = padded(stacked, (("gx", 1), ("gy", 2), ("gz", 3)), 2)

    def pair_block(scan_state, orbital):
        dens_wide = orbital[None] * vir_wide
        slopes = [derivative(dens_wide, dimension) for dimension in range(3)]
        dens_middle = trim_rim(dens_wide, 2)
        aligned = field_wide[4] * slopes[0] + field_wide[5] * slopes[1] + field_wide[6] * slopes[2]
        scalar = field_wide[1] * dens_middle + field_wide[2] * aligned
        fluxes = [
            scalar * field_wide[4 + dimension] + field_wide[3] * slopes[dimension]
            for dimension in range(3)
        ]
        divergence = derivative(fluxes[0], 0) + derivative(fluxes[1], 1) + derivative(fluxes[2], 2)
        return (
            scan_state,
            local_kernel * trim_rim(dens_middle, 2)
            + mixed_kernel * trim_rim(aligned, 2)
            - divergence,
        )

    unused_state, stacked_potential = lax.scan(pair_block, jnp.zeros((), jnp.float32), occ_wide)
    nocc = occupied.shape[0]
    cells = occupied.shape[1] * occupied.shape[2] * occupied.shape[3]
    potential = stacked_potential.reshape((nocc * nvir,) + occupied.shape[1:])
    devices_all = lax.axis_size("gx") * lax.axis_size("gy") * lax.axis_size("gz")
    total_cells = cells * devices_all
    flat_potential = potential.reshape((nocc * nvir, cells))
    occ_flat = occupied.reshape((nocc, cells))
    vir_flat = virtual.reshape((nvir, cells))
    own_rows = nocc * nvir // devices_all
    pair_index = lax.iota(jnp.int32, lax.axis_size(("gx", "gy", "gz")) * own_rows)
    occ_pick = (pair_index[:, None] // nvir == lax.iota(jnp.int32, nocc)[None, :]).astype(
        jnp.float32
    )
    vir_pick = (pair_index[:, None] % nvir == lax.iota(jnp.int32, nvir)[None, :]).astype(
        jnp.float32
    )
    occ_rows = jnp.dot(
        occ_pick, occ_flat, precision=lax.Precision.HIGHEST, preferred_element_type=jnp.float32
    )
    vir_rows = jnp.dot(
        vir_pick, vir_flat, precision=lax.Precision.HIGHEST, preferred_element_type=jnp.float32
    )
    casida = lax.psum_scatter(
        lax.dot_general(
            occ_rows * vir_rows,
            flat_potential,
            (((1,), (1,)), ((), ())),
            precision=lax.Precision.HIGHEST,
            preferred_element_type=jnp.float32,
        ),
        ("gx", "gy", "gz"),
        scatter_dimension=0,
        tiled=True,
    ) * (1.0 / total_cells)
    return (potential, casida)


def solution(mesh):
    placed = (
        P(None, "gx", "gy", "gz"),
        P(None, "gx", "gy", "gz"),
        P(None, "gx", "gy", "gz"),
        P(None, "gx", "gy", "gz"),
    )
    return jax.shard_map(
        on_device,
        mesh=mesh,
        in_specs=placed,
        out_specs=(P(None, "gx", "gy", "gz"), P(("gx", "gy", "gz"), None)),
        check_vma=False,
    )
```

profile of v0, /device:TPU:0, one launch (start us, length us, event | category | flops | bytes accessed | tf_op | source)
XLA Modules:
  0.0 404.4 jit_solution(8782214869207041111)
XLA Ops:
  9.3 1.9 collective-permute-start.7
  19.0 1.8 collective-permute-start.14
  20.8 2.1 collective-permute-start.15
  22.9 2.3 convolution_multiply_fusion
  28.9 6.4 %collective-permute-done.16 = f32[7,8,8,2]{3,2,1,0:T(8,128)S(1)} collective-permute-done((f32[7,8,8,2]{3,2,1,0:T(8,128)S(1)}, f32[7,8,8,2]{3,2,1,0:T(8,128)S(1)}, u32[]{:S(2)}, u32[]{:S(2)}) %collective-permute-start.16) | collective-permute-done | bytes 3616 | tf_op jit(solution)/shard_map/ppermute | solution.py:13
  35.4 4.1 %collective-permute-done.17 = f32[7,8,8,2]{3,2,1,0:T(8,128)S(1)} collective-permute-done((f32[7,8,8,2]{3,2,1,0:T(8,128)S(1)}, f32[7,8,8,2]{3,2,1,0:T(8,128)S(1)}, u32[]{:S(2)}, u32[]{:S(2)}) %collective-permute-start.17) | collective-permute-done | bytes 3616 | tf_op jit(solution)/shard_map/ppermute | solution.py:16
  43.7 2.8 collective-permute-start.9
  47.6 3.8 collective-permute-start.3
  51.4 5.1 %collective-permute-done.8 = f32[16,12,4,128]{3,0,2,1:T(8,128)S(1)} collective-permute-done((f32[16,12,4,128]{3,0,2,1:T(8,128)S(1)}, f32[16,12,4,128]{3,0,2,1:T(8,128)S(1)}, u32[]{:S(2)}, u32[]{:S(2)}) %collective-permute-start.8) | collective-permute-done | bytes 393248 | tf_op jit(solution)/shard_map/ppermute | solution.py:13
  56.4 8.5 %collective-permute-done.9 = f32[16,12,4,128]{3,0,2,1:T(8,128)S(1)} collective-permute-done((f32[16,12,4,128]{3,0,2,1:T(8,128)S(1)}, f32[16,12,4,128]{3,0,2,1:T(8,128)S(1)}, u32[]{:S(2)}, u32[]{:S(2)}) %collective-permute-start.9) | collective-permute-done | bytes 393248 | tf_op jit(solution)/shard_map/ppermute | solution.py:16
  69.2 1.6 copy.34
  71.5 2.0 collective-permute-done.2
  73.4 5.6 %collective-permute-done.3 = f32[16,12,4,128]{3,0,2,1:T(8,128)} collective-permute-done((f32[16,12,4,128]{3,0,2,1:T(8,128)S(1)}, f32[16,12,4,128]{3,0,2,1:T(8,128)}, u32[]{:S(2)}, u32[]{:S(2)}) %collective-permute-start.3) | collective-permute-done | bytes 393248 | tf_op jit(solution)/shard_map/ppermute | solution.py:16
  80.6 1.7 copy.31
  85.9 1.9 copy.26
  87.8 1.9 copy.27
  89.7 2.0 pad_maximum_fusion.1
  93.1 2.9 copy.19
  96.8 2.9 copy.20
  99.7 4.3 %pad_maximum_fusion = f32[16,12,12,136]{3,0,2,1:T(8,128)} fusion(f32[16,12,12,4]{3,0,2,1:T(8,128)} %copy.20, f32[16,12,4,128]{3,0,2,1:T(8,128)} %collective-permute-done.3, f32[16,12,4,128]{3,0,2,1:T(8,128)S(1)} %constant_dynamic-update-slice_fusion, f32[16,12,4,128]{3,0,2,1:T(8,128)} %collective-permute-done.2, f32[16,12,12,4]{3,0,2,1:T(8,128)} %copy.19), kind=kLoop, calls=%fused_computation.52 | loop fusion | flops 1253376 | bytes 2506752 | tf_op jit(solution)/shard_map/concatenate | solution.py:17
  104.0 150.3 %while.10 = (s32[]{:T(128)}, f32[16,16,4,4,128]{4,3,2,1,0:T(4,128)}, f32[1,4,4,128]{3,2,1,0:T(4,128)S(1)}, f32[16,12,12,136]{3,0,2,1:T(8,128)}, f32[16,12,12,136...) while((s32[]{:T(128)}, f32[16,16,4,4,128]{4,3,2,1,0:T(4,128)}, ...), condition=%wide.region_1.2_spmd, body=%wide.region_0.1_spmd.sunk | while | flops 5295106 | bytes 18330712 | solution.py:72
  107.8 3.4 multiply_add_fusion.7
  111.7 1.6 fusion.39
  117.2 3.4 multiply_add_fusion.7
  121.1 1.6 fusion.39
  126.6 3.4 multiply_add_fusion.7
  130.5 1.6 fusion.39
  136.0 3.4 multiply_add_fusion.7
  139.9 1.6 fusion.39
  145.4 3.4 multiply_add_fusion.7
  149.3 1.6 fusion.39
  154.8 3.4 multiply_add_fusion.7
  164.1 3.4 multiply_add_fusion.7
  173.5 3.4 multiply_add_fusion.7
  182.9 3.4 multiply_add_fusion.7
  186.9 1.6 fusion.39
  192.3 3.4 multiply_add_fusion.7
  196.3 1.6 fusion.39
  201.7 3.4 multiply_add_fusion.7
  211.1 3.4 multiply_add_fusion.7
  220.5 3.4 multiply_add_fusion.7
  229.9 3.4 multiply_add_fusion.7
  233.8 1.6 fusion.39
  239.3 3.4 multiply_add_fusion.7
  248.7 3.4 multiply_add_fusion.7
  254.3 3.2 reshape_reshape.3
  257.5 4.2 %fusion.33 = f32[256,256]{1,0:T(8,128)} fusion(f32[256,2048]{1,0:T(8,128)S(1)} %copy-done, f32[256,2048]{1,0:T(8,128)} %reshape_reshape.3), kind=kOutput, calls=%fused_computation.86 | convolution fusion | flops 1610612736 | bytes 4456448 | tf_op jit(solution)/shard_map/dot_general | solution.py:96
  261.7 134.5 %reduce-scatter.2.cloned.1.call-done = f32[8,256]{1,0:T(8,128)} async-done(((f32[256,256]{1,0:T(8,128)}), f32[8,256]{1,0:T(8,128)}) %reduce-scatter.2.cloned.1.call-update) | async-done | bytes 8208 | tf_op jit(solution)/shard_map/reduce_scatter | solution.py:95
  (172 shorter events, 113.9 us)
Async XLA Ops:
  7.2 11.7 %copy-start.2 = (f32[16,4,4,128]{3,2,1,0:T(4,128)S(1)}, f32[16,4,4,128]{3,2,1,0:T(4,128)}, u32[]{:S(2)}) copy-start(f32[16,4,4,128]{3,2,1,0:T(4,128)} %param.7) | copy-start | bytes 393220
  7.2 389.0 %reduce-scatter.2.cloned.1.call-start = ((), (), s32[]{:S(2)}) async-start(), calls=%async_computation.1 | async-start | bytes 270336 | tf_op jit(solution)/shard_map/reduce_scatter | solution.py:95
  8.8 31.9 %collective-permute-start.6 = (f32[16,4,4,128]{3,0,2,1:T(8,128)}, f32[16,4,4,128]{3,0,2,1:T(8,128)}, u32[]{:S(2)}, u32[]{:S(2)}) collective-permute-start(f32[16,4,4,128]{3,0,2,1:T(8,128)} %copy.21), channel_id=1, source_target_pairs={{0,8},{8,16},{16,24},{24,0},{1,9},{9,17},{17,25},{25,1},{2,10},{10... | collective-permute-start | bytes 393224 | tf_op jit(solution)/shard_map/ppermute | solution.py:13
  9.3 32.3 %collective-permute-start.7 = (f32[16,4,4,128]{3,0,2,1:T(8,128)}, f32[16,4,4,128]{3,0,2,1:T(8,128)}, u32[]{:S(2)}, u32[]{:S(2)}) collective-permute-start(f32[16,4,4,128]{3,0,2,1:T(8,128)} %copy.21), channel_id=1, source_target_pairs={{8,0},{16,8},{24,16},{0,24},{9,1},{17,9},{25,17},{1,25},{10,2},{18... | collective-permute-start | bytes 393224 | tf_op jit(solution)/shard_map/ppermute | solution.py:16
  12.8 6.2 %collective-permute-start.12 = (f32[7,2,4,128]{3,2,1,0:T(4,128)S(1)}, f32[7,2,4,128]{3,2,1,0:T(4,128)S(1)}, u32[]{:S(2)}, u32[]{:S(2)}) collective-permute-start(f32[7,2,4,128]{3,2,1,0:T(4,128)S(1)} %get-tuple-element.91), channel_id=1, source_target_pairs={{0,8},{8,16},{16,24},{24,0},{1,9},{9,17},{17,25},{25,1},{2,10},{10... | collective-permute-start | bytes 86024 | tf_op jit(solution)/shard_map/ppermute | solution.py:13
  13.5 5.4 %collective-permute-start.13 = (f32[7,2,4,128]{3,2,1,0:T(4,128)S(1)}, f32[7,2,4,128]{3,2,1,0:T(4,128)S(1)}, u32[]{:S(2)}, u32[]{:S(2)}) collective-permute-start(f32[7,2,4,128]{3,2,1,0:T(4,128)S(1)} %get-tuple-element.92), channel_id=1, source_target_pairs={{8,0},{16,8},{24,16},{0,24},{9,1},{17,9},{25,17},{1,25},{10,2},{18... | collective-permute-start | bytes 86024 | tf_op jit(solution)/shard_map/ppermute | solution.py:16
  16.2 30.3 %collective-permute-start = (f32[16,4,4,128]{3,0,2,1:T(8,128)}, f32[16,4,4,128]{3,0,2,1:T(8,128)}, u32[]{:S(2)}, u32[]{:S(2)}) collective-permute-start(f32[16,4,4,128]{3,0,2,1:T(8,128)} %copy.14), channel_id=1, source_target_pairs={{0,8},{8,16},{16,24},{24,0},{1,9},{9,17},{17,25},{25,1},{2,10},{10... | collective-permute-start | bytes 393224 | tf_op jit(solution)/shard_map/ppermute | solution.py:13
  19.0 6.2 %collective-permute-start.14 = (f32[7,8,2,128]{3,2,1,0:T(2,128)S(1)}, f32[7,8,2,128]{3,2,1,0:T(2,128)S(1)}, u32[]{:S(2)}, u32[]{:S(2)}) collective-permute-start(f32[7,8,2,128]{3,2,1,0:T(2,128)S(1)} %get-tuple-element.89), channel_id=1, source_target_pairs={{0,2},{2,4},{4,6},{6,0},{1,3},{3,5},{5,7},{7,1},{8,10},{10,12},{12... | collective-permute-start | bytes 172040 | tf_op jit(solution)/shard_map/ppermute | solution.py:13
  20.8 8.1 %copy-start.4 = (f32[4,4,4,128]{3,2,1,0:T(4,128)S(1)}, f32[4,4,4,128]{3,2,1,0:T(4,128)}, u32[]{:S(2)}) copy-start(f32[4,4,4,128]{3,2,1,0:T(4,128)} %param.8) | copy-start | bytes 98308
  20.8 5.8 %collective-permute-start.15 = (f32[7,8,2,128]{3,2,1,0:T(2,128)S(1)}, f32[7,8,2,128]{3,2,1,0:T(2,128)S(1)}, u32[]{:S(2)}, u32[]{:S(2)}) collective-permute-start(f32[7,8,2,128]{3,2,1,0:T(2,128)S(1)} %get-tuple-element.90), channel_id=1, source_target_pairs={{2,0},{4,2},{6,4},{0,6},{3,1},{5,3},{7,5},{1,7},{10,8},{12,10},{14... | collective-permute-start | bytes 172040 | tf_op jit(solution)/shard_map/ppermute | solution.py:16
  25.2 22.2 %copy-start.3 = (f32[16,4,4,128]{3,2,1,0:T(4,128)S(1)}, f32[16,4,4,128]{3,2,1,0:T(4,128)}, u32[]{:S(2)}) copy-start(f32[16,4,4,128]{3,2,1,0:T(4,128)} %param.6) | copy-start | bytes 393220
  26.8 8.5 %collective-permute-start.16 = (f32[7,8,8,2]{3,2,1,0:T(8,128)S(1)}, f32[7,8,8,2]{3,2,1,0:T(8,128)S(1)}, u32[]{:S(2)}, u32[]{:S(2)}) collective-permute-start(f32[7,8,8,2]{3,2,1,0:T(8,128)S(1)} %get-tuple-element.87), channel_id=1, source_target_pairs={{0,1},{1,0},{2,3},{3,2},{4,5},{5,4},{6,7},{7,6},{8,9},{9,8},{10,11... | collective-permute-start | bytes 10760 | tf_op jit(solution)/shard_map/ppermute | solution.py:13
  28.3 11.2 %collective-permute-start.17 = (f32[7,8,8,2]{3,2,1,0:T(8,128)S(1)}, f32[7,8,8,2]{3,2,1,0:T(8,128)S(1)}, u32[]{:S(2)}, u32[]{:S(2)}) collective-permute-start(f32[7,8,8,2]{3,2,1,0:T(8,128)S(1)} %get-tuple-element.88), channel_id=1, source_target_pairs={{1,0},{0,1},{3,2},{2,3},{5,4},{4,5},{7,6},{6,7},{9,8},{8,9},{11,10... | collective-permute-start | bytes 10760 | tf_op jit(solution)/shard_map/ppermute | solution.py:16
  35.4 12.1 %collective-permute-start.1 = (f32[16,4,4,128]{3,0,2,1:T(8,128)}, f32[16,4,4,128]{3,0,2,1:T(8,128)S(1)}, u32[]{:S(2)}, u32[]{:S(2)}) collective-permute-start(f32[16,4,4,128]{3,0,2,1:T(8,128)} %copy.14), channel_id=1, source_target_pairs={{8,0},{16,8},{24,16},{0,24},{9,1},{17,9},{25,17},{1,25},{10,2},{18... | collective-permute-start | bytes 393224 | tf_op jit(solution)/shard_map/ppermute | solution.py:16
  42.6 13.8 %collective-permute-start.8 = (f32[16,12,4,128]{3,0,2,1:T(8,128)S(1)}, f32[16,12,4,128]{3,0,2,1:T(8,128)S(1)}, u32[]{:S(2)}, u32[]{:S(2)}) collective-permute-start(f32[16,12,4,128]{3,0,2,1:T(8,128)S(1)} %constant_dynamic-update-slice_fusion.3), channel_id=1, source_target_pairs={{0,2},{2,4},{4,6},{6,0},{1,3},{3,5},{5,7},{7,1},{8,10},{10,12},{12... | collective-permute-start | bytes 1179656 | tf_op jit(solution)/shard_map/ppermute | solution.py:13
  43.7 21.3 %collective-permute-start.9 = (f32[16,12,4,128]{3,0,2,1:T(8,128)S(1)}, f32[16,12,4,128]{3,0,2,1:T(8,128)S(1)}, u32[]{:S(2)}, u32[]{:S(2)}) collective-permute-start(f32[16,12,4,128]{3,0,2,1:T(8,128)S(1)} %constant_dynamic-update-slice_fusion.3), channel_id=1, source_target_pairs={{2,0},{4,2},{6,4},{0,6},{3,1},{5,3},{7,5},{1,7},{10,8},{12,10},{14... | collective-permute-start | bytes 1179656 | tf_op jit(solution)/shard_map/ppermute | solution.py:16
  47.5 26.0 %collective-permute-start.2 = (f32[16,12,4,128]{3,0,2,1:T(8,128)S(1)}, f32[16,12,4,128]{3,0,2,1:T(8,128)}, u32[]{:S(2)}, u32[]{:S(2)}) collective-permute-start(f32[16,12,4,128]{3,0,2,1:T(8,128)S(1)} %constant_dynamic-update-slice_fusion), channel_id=1, source_target_pairs={{0,2},{2,4},{4,6},{6,0},{1,3},{3,5},{5,7},{7,1},{8,10},{10,12},{12... | collective-permute-start | bytes 1179656 | tf_op jit(solution)/shard_map/ppermute | solution.py:13
  47.6 31.5 %collective-permute-start.3 = (f32[16,12,4,128]{3,0,2,1:T(8,128)S(1)}, f32[16,12,4,128]{3,0,2,1:T(8,128)}, u32[]{:S(2)}, u32[]{:S(2)}) collective-permute-start(f32[16,12,4,128]{3,0,2,1:T(8,128)S(1)} %constant_dynamic-update-slice_fusion), channel_id=1, source_target_pairs={{2,0},{4,2},{6,4},{0,6},{3,1},{5,3},{7,5},{1,7},{10,8},{12,10},{14... | collective-permute-start | bytes 1179656 | tf_op jit(solution)/shard_map/ppermute | solution.py:16
  64.9 0.7 copy-start.1
  67.8 18.2 %collective-permute-start.10 = (f32[16,12,12,4]{0,3,2,1:T(4,128)}, f32[16,12,12,4]{0,3,2,1:T(4,128)}, u32[]{:S(2)}, u32[]{:S(2)}) collective-permute-start(f32[16,12,12,4]{0,3,2,1:T(4,128)} %copy.33), channel_id=1, source_target_pairs={{0,1},{1,0},{2,3},{3,2},{4,5},{5,4},{6,7},{7,6},{8,9},{9,8},{10,11... | collective-permute-start | bytes 110600 | tf_op jit(solution)/shard_map/ppermute | solution.py:13
  70.8 17.0 %collective-permute-start.11 = (f32[16,12,12,4]{0,3,2,1:T(4,128)}, f32[16,12,12,4]{0,3,2,1:T(4,128)}, u32[]{:S(2)}, u32[]{:S(2)}) collective-permute-start(f32[16,12,12,4]{0,3,2,1:T(4,128)} %copy.34), channel_id=1, source_target_pairs={{1,0},{0,1},{3,2},{2,3},{5,4},{4,5},{7,6},{6,7},{9,8},{8,9},{11,10... | collective-permute-start | bytes 110600 | tf_op jit(solution)/shard_map/ppermute | solution.py:16
  82.3 10.8 %collective-permute-start.4 = (f32[16,12,12,4]{0,3,2,1:T(4,128)}, f32[16,12,12,4]{0,3,2,1:T(4,128)}, u32[]{:S(2)}, u32[]{:S(2)}) collective-permute-start(f32[16,12,12,4]{0,3,2,1:T(4,128)} %copy.31), channel_id=1, source_target_pairs={{0,1},{1,0},{2,3},{3,2},{4,5},{5,4},{6,7},{7,6},{8,9},{9,8},{10,11... | collective-permute-start | bytes 110600 | tf_op jit(solution)/shard_map/ppermute | solution.py:13
  85.4 11.4 %collective-permute-start.5 = (f32[16,12,12,4]{0,3,2,1:T(4,128)}, f32[16,12,12,4]{0,3,2,1:T(4,128)}, u32[]{:S(2)}, u32[]{:S(2)}) collective-permute-start(f32[16,12,12,4]{0,3,2,1:T(4,128)} %copy.32), channel_id=1, source_target_pairs={{1,0},{0,1},{3,2},{2,3},{5,4},{4,5},{7,6},{6,7},{9,8},{8,9},{11,10... | collective-permute-start | bytes 110600 | tf_op jit(solution)/shard_map/ppermute | solution.py:16
  254.3 3.2 copy-start
Sparse Core Ops, SparseCore 0:
  261.8 134.3 reduce-scatter.1
where the time goes:
time: 407 us; the launch traced here: 404 us
  waiting for transfers between devices  168 us (41%)
  other arithmetic  137 us (34%)
  local copies, waits for them, and re-layouts  53.4 us (13%)
  starting transfers between devices  22.7 us (6%)
  between operations  14.3 us (4%)
  matrix products  7.54 us (2%)
    reduce_scatter x1, waiting for transfers between devices, on_device(): lax.psum_scatter(lax.dot_general(occ_rows * vir_rows, flat_potential, (((...  135 us
    add x32, other arithmetic, pair_block(): scalar * field_wide[4 + dimension] + field_wide[3] * slopes[dimension]  62.8 us
    dynamic_update_slice x16, other arithmetic, on_device(): lax.scan(pair_block, jnp.zeros((), jnp.float32), occ_wide)  26.2 us
    dynamic_slice x32, local copies, waits for them, and re-layouts, on_device(): lax.scan(pair_block, jnp.zeros((), jnp.float32), occ_wide)  22.4 us
    ppermute x9, waiting for transfers between devices, padded(): lax.ppermute(lax.slice_in_dim(block, 0, width, axis=dim), axis, backward)  20.4 us
    mul x16, other arithmetic, pair_block(): field_wide[5] * slopes[1]  16.4 us
    mul x16, other arithmetic, pair_block(): field_wide[4] * slopes[0] + field_wide[5] * slopes[1]  14.8 us
    ppermute x9, waiting for transfers between devices, padded(): lax.ppermute(lax.slice_in_dim(block, block.shape[dim] - width, None, axis...  13.5 us
  transfers between devices with their start and end apart: 19, of which 9 were waited for; matrix products, arithmetic and copies ran while one was open for 8% of the time, Pallas kernels for 0%

commit v1 on v0

v1 whole, which is shorter than its diff:
```python
import jax
import jax.numpy as jnp
from jax import lax
from jax.experimental import pallas as pl
from jax.experimental.pallas import tpu as pltpu
from jax.sharding import PartitionSpec as P

REACH = 4
RIM = 2
SHIFTS = (1, -1, 2, -2)


def ring(count, step):
    return [(i, (i + step) % count) for i in range(count)]


def pack_kernel(nx, ny, occ, vir, fields, grad, tile_ref, edge_ref):
    cols = nx * ny
    lanes = tile_ref.shape[-1]
    nvir = vir.shape[0] // cols
    nocc = occ.shape[0] // cols
    half = edge_ref.shape[0] // 2
    per = lanes // REACH
    lane = lax.broadcasted_iota(jnp.int32, tile_ref.shape[1:], 1)
    first = [jnp.zeros(tile_ref.shape[1:], jnp.float32) for _ in range(half)]
    last = [jnp.zeros(tile_ref.shape[1:], jnp.float32) for _ in range(half)]
    used = nvir + nocc + 7
    for c in range(cols):
        tile_ref[c, 0:nvir, :] = vir[pl.ds(c, nvir, stride=cols), :]
        tile_ref[c, nvir : nvir + nocc, :] = occ[pl.ds(c, nocc, stride=cols), :]
        rows = [fields[k * cols + c : k * cols + c + 1, :] for k in range(3)]
        rows.append(fields[3 * cols + c : 3 * cols + c + 1, :] * (1.0 / 144.0))
        rows += [grad[k * cols + c : k * cols + c + 1, :] * (1.0 / 12.0) for k in range(3)]
        for k, row in enumerate(rows):
            tile_ref[c, nvir + nocc + k : nvir + nocc + k + 1, :] = row
        if used < tile_ref.shape[1]:
            tile_ref[c, used:, :] = jnp.zeros((tile_ref.shape[1] - used, lanes), jnp.float32)
        whole = tile_ref[c]
        at, off = c // per, (c % per) * REACH
        here = (lane >= off) & (lane < off + REACH)
        first[at] = jnp.where(here, pltpu.roll(whole, off, 1), first[at])
        last[at] = jnp.where(here, pltpu.roll(whole, (off + REACH) % lanes, 1), last[at])
    for k in range(half):
        edge_ref[k] = first[k]
        edge_ref[half + k] = last[k]


def main_kernel(
    nx, ny, nvir, nocc, scale,
    tile, ends, xlo, xhi, ylo, yhi, clo, chi,
    pot_ref, gram_ref,
    halo, zmid, zhalo, dens, dens_h, flux0, flux1, flux2, flux2h, base,
    dens_hi, dens_lo, pot_hi, pot_lo,
):
    cols = nx * ny
    lanes = tile.shape[-1]
    rows = tile.shape[1]
    orbs = nvir + nocc
    half = ends.shape[0] // 2
    per = lanes // REACH

    def column(x, y):
        if 0 <= x < nx and 0 <= y < ny:
            return tile, x * ny + y
        if 0 <= y < ny:
            return (xlo, (x + REACH) * ny + y) if x < 0 else (xhi, (x - nx) * ny + y)
        if 0 <= x < nx:
            return (ylo, x * REACH + y + REACH) if y < 0 else (yhi, x * REACH + y - ny)
        at = x + RIM if x < 0 else RIM + x - nx
        return (clo, at * RIM + y + RIM) if y < 0 else (chi, at * RIM + y - ny)

    def ends_of(x, y):
        if 0 <= x < nx and 0 <= y < ny:
            return ends, 0, x * ny + y
        if 0 <= y < ny:
            return (xlo, REACH * ny, (x + nx) * ny + y) if x < 0 else (xhi, REACH * ny, (x - nx) * ny + y)
        return (ylo, nx * REACH, x * ny + y + ny) if y < 0 else (yhi, nx * REACH, x * ny + y - ny)

    centre = [(x, y) for x in range(nx) for y in range(ny)]
    cross = list(centre)
    cross += [(x, y) for x in (-2, -1, nx, nx + 1) for y in range(ny)]
    cross += [(x, y) for y in (-2, -1, ny, ny + 1) for x in range(nx)]
    cross_at = {c: k for k, c in enumerate(cross)}
    wide = list(cross)
    wide += [(x, y) for x in (-4, -3, nx + 2, nx + 3) for y in range(ny)]
    wide += [(x, y) for y in (-4, -3, ny + 2, ny + 3) for x in range(nx)]
    wide += [(x, y) for x in (-2, -1, nx, nx + 1) for y in (-2, -1, ny, ny + 1)]
    wide_at = {c: k for k, c in enumerate(wide)}

    def move(mid, out, by):
        lane = lax.broadcasted_iota(jnp.int32, mid.shape, 1)
        a = pltpu.roll(mid, (-by) % lanes, 1)
        b = pltpu.roll(out, (-by) % lanes, 1)
        wraps = lane >= lanes - by if by > 0 else lane < -by
        return jnp.where(wraps, b, a), jnp.where(wraps, a, b)

    for k, (x, y) in enumerate(cross):
        ref, start, c = ends_of(x, y)
        at, off = c // per, (c % per) * REACH
        lane = lax.broadcasted_iota(jnp.int32, (rows, lanes), 1)
        above = pltpu.roll(ref[start + at], (-off) % lanes, 1)
        below = pltpu.roll(ref[start + half + at], (lanes - REACH - off) % lanes, 1)
        out = jnp.where(lane < lanes // 2, above, below)
        halo[k] = out
        ref, c = column(x, y)
        for s, by in enumerate(SHIFTS):
            mid_s, out_s = move(ref[c, 0:orbs, :], out[0:orbs], by)
            gain = 8.0 if abs(by) == 1 else 1.0
            zmid[k, s, 0:nvir, :] = mid_s[0:nvir] * gain
            zmid[k, s, nvir:, :] = mid_s[nvir:]
            if k < cols:
                zhalo[k, s, 0:nvir, :] = out_s[0:nvir] * gain
                zhalo[k, s, nvir:, :] = out_s[nvir:]

    def stencil(p1, m1, p2, m2):
        return 8.0 * (p1 - m1) - (p2 - m2)

    def spread(row):
        return jnp.broadcast_to(row, (nvir, lanes))

    def per_orbital(i, carry):
        row = nvir + i
        pair0 = pl.multiple_of(i * nvir, nvir)
        for k, (x, y) in enumerate(wide):
            ref, c = column(x, y)
            dens[k] = spread(ref[c, pl.ds(row, 1), :]) * ref[c, 0:nvir, :]
        for k in range(len(cross)):
            dens_h[k] = spread(halo[k, pl.ds(row, 1), :]) * halo[k, 0:nvir, :]

        def slope_z(store, k):
            p1, m1, p2, m2 = [
                spread(store[k, s, pl.ds(row, 1), :]) * store[k, s, 0:nvir, :] for s in range(4)
            ]
            return (p1 - m1) - (p2 - m2)

        def respond(d, s0, s1, s2, field):
            g = [field(4 + j) for j in range(3)]
            aligned = g[0] * s0 + g[1] * s1 + g[2] * s2
            scalar = field(1) * d + field(2) * aligned
            return aligned, scalar, g

        for k, (x, y) in enumerate(cross):
            s0 = stencil(*[dens[wide_at[(x + b, y)]] for b in SHIFTS])
            s1 = stencil(*[dens[wide_at[(x, y + b)]] for b in SHIFTS])
            s2 = slope_z(zmid, k)
            ref, c = column(x, y)

            def field(j):
                return spread(ref[c, orbs + j : orbs + j + 1, :])

            d = dens[k]
            aligned, scalar, g = respond(d, s0, s1, s2, field)
            if 0 <= y < ny:
                flux0[(x + RIM) * ny + y] = scalar * g[0] + field(3) * s0
            if 0 <= x < nx:
                flux1[x * (ny + 2 * RIM) + y + RIM] = scalar * g[1] + field(3) * s1
            if k < cols:
                flux2[k] = scalar * g[2] + field(3) * s2
                base[k] = field(0) * d + field(1) * aligned
                s0 = stencil(*[dens_h[cross_at[(x + b, y)]] for b in SHIFTS])
                s1 = stencil(*[dens_h[cross_at[(x, y + b)]] for b in SHIFTS])
                s2 = slope_z(zhalo, k)

                def field_h(j):
                    return spread(halo[k, orbs + j : orbs + j + 1, :])

                aligned, scalar, g = respond(dens_h[k], s0, s1, s2, field_h)
                flux2h[k] = scalar * g[2] + field_h(3) * s2
        for k, (x, y) in enumerate(centre):
            mid, out = flux2[k], flux2h[k]
            total = stencil(*[move(mid, out, b)[0] for b in SHIFTS])
            total += stencil(*[flux0[(x + RIM + b) * ny + y] for b in SHIFTS])
            total += stencil(*[flux1[x * (ny + 2 * RIM) + y + RIM + b] for b in SHIFTS])
            pot = base[k] - total
            pot_ref[pl.ds(pair0 * cols + k, nvir, stride=cols), :] = pot
            there = (pl.ds(pair0, nvir), slice(k * lanes, (k + 1) * lanes))
            top = pot.astype(jnp.bfloat16)
            pot_hi[there] = top
            pot_lo[there] = (pot - top.astype(jnp.float32)).astype(jnp.bfloat16)
            d = dens[k]
            top = d.astype(jnp.bfloat16)
            dens_hi[there] = top
            dens_lo[there] = (d - top.astype(jnp.float32)).astype(jnp.bfloat16)
        return carry

    lax.fori_loop(0, nocc, per_orbital, 0)

    def product(a, b):
        return lax.dot_general(
            a[...], b[...], (((1,), (1,)), ((), ())), preferred_element_type=jnp.float32
        )

    gram = product(dens_hi, pot_lo) + product(dens_lo, pot_hi) + product(dens_hi, pot_hi)
    gram_ref[...] = gram * scale


def on_device(occupied, virtual, kernel_fields, density_grad):
    nocc, nx, ny, nz = occupied.shape
    nvir = virtual.shape[0]
    cols = nx * ny
    rows = -(-(nocc + nvir + 7) // 8) * 8
    half = -(-cols * REACH // nz)
    f32 = jnp.float32
    vmem = pl.BlockSpec(memory_space=pltpu.VMEM)
    axes = ("gx", "gy", "gz")
    devices = lax.axis_size(axes)

    def flat(values):
        return values.reshape((values.shape[0] * cols, nz))

    tile, edges = pl.pallas_call(
        lambda *refs: pack_kernel(nx, ny, *refs),
        out_shape=(
            jax.ShapeDtypeStruct((cols, rows, nz), f32),
            jax.ShapeDtypeStruct((2 * half, rows, nz), f32),
        ),
        in_specs=[vmem] * 4,
        out_specs=(vmem, vmem),
    )(flat(occupied), flat(virtual), flat(kernel_fields), flat(density_grad))

    gz = lax.axis_size("gz")
    if gz == 2:
        ends = lax.ppermute(edges, "gz", ring(gz, 1))
    else:
        ends = jnp.concatenate(
            [
                lax.ppermute(edges[:half], "gz", ring(gz, -1)),
                lax.ppermute(edges[half:], "gz", ring(gz, 1)),
            ]
        )
    gx, gy = lax.axis_size("gx"), lax.axis_size("gy")
    grid = tile.reshape((nx, ny, rows, nz))

    def with_ends(block):
        return jnp.concatenate([block.reshape((-1, rows, nz)), ends])

    xlo = lax.ppermute(with_ends(grid[nx - REACH :]), "gx", ring(gx, 1))
    xhi = lax.ppermute(with_ends(grid[:REACH]), "gx", ring(gx, -1))
    ylo = lax.ppermute(with_ends(grid[:, ny - REACH :]), "gy", ring(gy, 1))
    yhi = lax.ppermute(with_ends(grid[:, :REACH]), "gy", ring(gy, -1))
    rims = jnp.concatenate(
        [xlo[(REACH - RIM) * ny : REACH * ny], xhi[: RIM * ny]]
    ).reshape((2 * RIM, ny, rows, nz))
    clo = lax.ppermute(rims[:, ny - RIM :].reshape((-1, rows, nz)), "gy", ring(gy, 1))
    chi = lax.ppermute(rims[:, :RIM].reshape((-1, rows, nz)), "gy", ring(gy, -1))

    n_cross = cols + 4 * (nx + ny)
    n_wide = n_cross + 4 * (nx + ny) + 16
    pairs = nocc * nvir
    block = (nvir, nz)
    scratch = [
        pltpu.VMEM((n_cross, rows, nz), f32),
        pltpu.VMEM((n_cross, 4, nvir + nocc, nz), f32),
        pltpu.VMEM((cols, 4, nvir + nocc, nz), f32),
        pltpu.VMEM((n_wide,) + block, f32),
        pltpu.VMEM((n_cross,) + block, f32),
        pltpu.VMEM(((nx + 2 * RIM) * ny,) + block, f32),
        pltpu.VMEM((nx * (ny + 2 * RIM),) + block, f32),
        pltpu.VMEM((cols,) + block, f32),
        pltpu.VMEM((cols,) + block, f32),
        pltpu.VMEM((cols,) + block, f32),
    ] + [pltpu.VMEM((pairs, cols * nz), jnp.bfloat16)] * 4
    scale = 1.0 / (cols * nz * devices)
    potential, gram = pl.pallas_call(
        lambda *refs: main_kernel(nx, ny, nvir, nocc, scale, *refs),
        out_shape=(
            jax.ShapeDtypeStruct((pairs * cols, nz), f32),
            jax.ShapeDtypeStruct((pairs, pairs), f32),
        ),
        in_specs=[vmem] * 8,
        out_specs=(vmem, vmem),
        scratch_shapes=scratch,
        compiler_params=pltpu.CompilerParams(vmem_limit_bytes=56 << 20),
    )(tile, ends, xlo, xhi, ylo, yhi, clo, chi)

    parts = lax.all_to_all(gram.reshape((devices, pairs // devices, pairs)), axes, 0, 0)
    casida = jnp.sum(parts, axis=0)
    return potential.reshape((pairs, nx, ny, nz)), casida


def solution(mesh):
    placed = P(None, "gx", "gy", "gz")
    return jax.shard_map(
        on_device,
        mesh=mesh,
        in_specs=(placed,) * 4,
        out_specs=(placed, P(("gx", "gy", "gz"), None)),
        check_vma=False,
    )
```

time: 407 us -> 74.2 us (0.18)
  waiting for transfers between devices: 168 us -> 21.8 us
  other arithmetic: 137 us -> 0.66 us
  local copies, waits for them, and re-layouts: 53.4 us -> 1.72 us
  Pallas kernels: 0 us -> 22 us
  blocking collectives: 0 us -> 15.3 us
  between operations: 14.3 us -> 0.71 us
  starting transfers between devices: 22.7 us -> 11.7 us
  matrix products: 7.54 us -> 0 us
    reduce_scatter x1 -> x0, waiting for transfers between devices: 135 us -> none  [on_device(): lax.psum_scatter(lax.dot_general(occ_rows * vir_rows, flat_potential, (((...]
    add x32 -> x0, other arithmetic: 62.8 us -> none  [pair_block(): scalar * field_wide[4 + dimension] + field_wide[3] * slopes[dimension]]
    mul x49 -> x0, other arithmetic: 39.4 us -> none  [the longest x16 16.4 us: pair_block(): field_wide[5] * slopes[1]]
    dynamic_update_slice x16 -> x0, other arithmetic: 26.2 us -> none  [on_device(): lax.scan(pair_block, jnp.zeros((), jnp.float32), occ_wide)]
    dynamic_slice x32 -> x0, local copies, waits for them, and re-layouts: 22.4 us -> none  [on_device(): lax.scan(pair_block, jnp.zeros((), jnp.float32), occ_wide)]
    pallas_call x0 -> x2, Pallas kernels: none -> 22 us  [the longest x1 20.1 us: on_device(): pl.pallas_call(lambda *refs: main_kernel(nx, ny, nvir, nocc, scale, *refs...]
    all_to_all x0 -> x1, blocking collectives: none -> 15.3 us  [on_device(): lax.all_to_all(gram.reshape((devices, pairs // devices, pairs)), axes, 0, 0)]
    ppermute x18 -> x7, waiting for transfers between devices: 33.9 us -> 21.8 us  [the longest x1 7.07 us: on_device(): ylo = lax.ppermute(with_ends(grid[:, ny - REACH:]), 'gy', ring(gy, 1))]
  transfers between devices with their start and end apart: 19 -> 7, of which waited for: 9 -> 6; matrix products, arithmetic and copies ran while one was open for 8% -> 1% of each run, Pallas kernels for 0% -> 0%
where the time goes in v1:
time: 74.2 us; the launch traced here: 73.9 us
  Pallas kernels  22 us (30%)
  waiting for transfers between devices  21.8 us (29%)
  blocking collectives  15.3 us (21%)
  starting transfers between devices  11.7 us (16%)
  local copies, waits for them, and re-layouts  1.72 us (2%)
    pallas_call x1, Pallas kernels, on_device(): pl.pallas_call(lambda *refs: main_kernel(nx, ny, nvir, nocc, scale, *refs...  20.1 us
    all_to_all x1, blocking collectives, on_device(): lax.all_to_all(gram.reshape((devices, pairs // devices, pairs)), axes, 0, 0)  15.3 us
    ppermute x1, waiting for transfers between devices, on_device(): ylo = lax.ppermute(with_ends(grid[:, ny - REACH:]), 'gy', ring(gy, 1))  7.07 us
    ppermute x1, starting transfers between devices, on_device(): yhi = lax.ppermute(with_ends(grid[:, :REACH]), 'gy', ring(gy, -1))  4.11 us
    ppermute x1, waiting for transfers between devices, on_device(): lax.ppermute(rims[:, :RIM].reshape((-1, rows, nz)), 'gy', ring(gy, -1))  3.6 us
    ppermute x1, waiting for transfers between devices, on_device(): lax.ppermute(rims[:, ny - RIM:].reshape((-1, rows, nz)), 'gy', ring(gy, 1))  3.51 us
    ppermute x1, waiting for transfers between devices, on_device(): xhi = lax.ppermute(with_ends(grid[:REACH]), 'gx', ring(gx, -1))  3.45 us
    ppermute x1, starting transfers between devices, on_device(): ends = lax.ppermute(edges, 'gz', ring(gz, 1))  3 us
  transfers between devices with their start and end apart: 7, of which 6 were waited for; matrix products, arithmetic and copies ran while one was open for 1% of the time, Pallas kernels for 0%

profile of v1, /device:TPU:0, one launch (start us, length us, event | category | flops | bytes accessed | tf_op | source)
XLA Modules:
  0.0 73.9 jit_solution(4675534037350373746)
XLA Ops:
  0.6 1.9 %shard_map.59 = (f32[16,40,128]{2,1,0:T(8,128)}, f32[2,40,128]{2,1,0:T(8,128)}) custom-call(f32[256,128]{1,0:T(8,128)} %bitcast.13, f32[256,128]{1,0:T(8,128)} %bitcast.14, f32[64,128]{1,0:T(8,128)} %bitcast.15, f32[48,128]{1,0:T(8,128)} %bitcast.16), custom_call_target="tpu_custom_call" | custom-call | tf_op jit(solution)/shard_map/pallas_call | solution.py:211
  2.5 3.0 %collective-permute-start = (f32[2,40,128]{2,1,0:T(8,128)}, f32[2,40,128]{2,1,0:T(8,128)S(1)}, u32[]{:S(2)}, u32[]{:S(2)}) collective-permute-start(f32[2,40,128]{2,1,0:T(8,128)} %get-tuple-element.7), channel_id=1, source_target_pairs={{0,1},{1,0},{2,3},{3,2},{4,5},{5,4},{6,7},{7,6},{8,9},{9,8},{10,11... | collective-permute-start | bytes 122888 | tf_op jit(solution)/shard_map/ppermute | solution.py:223
  5.5 1.0 %constant_dynamic-update-slice_fusion.1 = f32[18,40,128]{2,1,0:T(8,128)S(1)} fusion(f32[16,40,128]{2,1,0:T(8,128)} %get-tuple-element.6.refs_0_), kind=kLoop, calls=%fused_computation.2 | loop fusion | bytes 655360
  6.5 1.2 %collective-permute-done.refs_1_ = f32[2,40,128]{2,1,0:T(8,128)S(1)} collective-permute-done((f32[2,40,128]{2,1,0:T(8,128)}, f32[2,40,128]{2,1,0:T(8,128)S(1)}, u32[]{:S(2)}, u32[]{:S(2)}) %collective-permute-start) | collective-permute-done | bytes 40992 | tf_op jit(solution)/shard_map/ppermute | solution.py:223
  7.7 0.0 copy-start.6
  7.7 0.3 collective-permute-start.2
  8.0 0.2 collective-permute-start.1
  8.2 4.1 %collective-permute-start.4 = (f32[18,40,128]{2,1,0:T(8,128)S(1)}, f32[18,40,128]{2,1,0:T(8,128)S(1)}, u32[]{:S(2)}, u32[]{:S(2)}) collective-permute-start(f32[18,40,128]{2,1,0:T(8,128)S(1)} %constant_dynamic-update-slice_fusion), channel_id=1, source_target_pairs={{0,6},{2,0},{4,2},{6,4},{1,7},{3,1},{5,3},{7,5},{8,14},{10,8},{12,... | collective-permute-start | bytes 1105928 | tf_op jit(solution)/shard_map/ppermute | solution.py:240
  12.3 0.0 collective-permute-start.3
  12.3 3.5 %collective-permute-done.2.refs_3_ = f32[18,40,128]{2,1,0:T(8,128)S(1)} collective-permute-done((f32[18,40,128]{2,1,0:T(8,128)S(1)}, f32[18,40,128]{2,1,0:T(8,128)S(1)}, u32[]{:S(2)}, u32[]{:S(2)}) %collective-permute-start.2) | collective-permute-done | bytes 368672 | tf_op jit(solution)/shard_map/ppermute | solution.py:238
  15.8 0.0 copy-start
  15.8 3.0 %collective-permute-done.1.refs_2_ = f32[18,40,128]{2,1,0:T(8,128)S(1)} collective-permute-done((f32[18,40,128]{2,1,0:T(8,128)S(1)}, f32[18,40,128]{2,1,0:T(8,128)S(1)}, u32[]{:S(2)}, u32[]{:S(2)}) %collective-permute-start.1) | collective-permute-done | bytes 368672 | tf_op jit(solution)/shard_map/ppermute | solution.py:237
  18.8 0.0 copy-start.1
  18.8 2.0 %collective-permute-start.5 = (f32[8,40,128]{2,1,0:T(8,128)S(1)}, f32[8,40,128]{2,1,0:T(8,128)S(1)}, u32[]{:S(2)}, u32[]{:S(2)}) collective-permute-start(f32[8,40,128]{2,1,0:T(8,128)S(1)} %bitcast.12), channel_id=1, source_target_pairs={{0,2},{2,4},{4,6},{6,0},{1,3},{3,5},{5,7},{7,1},{8,10},{10,12},{12... | collective-permute-start | bytes 491528 | tf_op jit(solution)/shard_map/ppermute | solution.py:244
  20.8 2.1 %collective-permute-start.6 = (f32[8,40,128]{2,1,0:T(8,128)S(1)}, f32[8,40,128]{2,1,0:T(8,128)S(1)}, u32[]{:S(2)}, u32[]{:S(2)}) collective-permute-start(f32[8,40,128]{2,1,0:T(8,128)S(1)} %bitcast.11), channel_id=1, source_target_pairs={{0,6},{2,0},{4,2},{6,4},{1,7},{3,1},{5,3},{7,5},{8,14},{10,8},{12,... | collective-permute-start | bytes 491528 | tf_op jit(solution)/shard_map/ppermute | solution.py:245
  22.9 0.0 collective-permute-done.4.refs_5_
  22.9 0.0 copy-start.2
  22.9 7.1 %collective-permute-done.3.refs_4_ = f32[18,40,128]{2,1,0:T(8,128)S(1)} collective-permute-done((f32[18,40,128]{2,1,0:T(8,128)S(1)}, f32[18,40,128]{2,1,0:T(8,128)S(1)}, u32[]{:S(2)}, u32[]{:S(2)}) %collective-permute-start.3) | collective-permute-done | bytes 368672 | tf_op jit(solution)/shard_map/ppermute | solution.py:239
  30.0 0.0 copy-start.3
  30.0 3.5 %collective-permute-done.5.refs_6_ = f32[8,40,128]{2,1,0:T(8,128)S(1)} collective-permute-done((f32[8,40,128]{2,1,0:T(8,128)S(1)}, f32[8,40,128]{2,1,0:T(8,128)S(1)}, u32[]{:S(2)}, u32[]{:S(2)}) %collective-permute-start.5) | collective-permute-done | bytes 163872 | tf_op jit(solution)/shard_map/ppermute | solution.py:244
  33.5 0.0 copy-start.4
  33.5 3.6 %collective-permute-done.6.refs_7_ = f32[8,40,128]{2,1,0:T(8,128)S(1)} collective-permute-done((f32[8,40,128]{2,1,0:T(8,128)S(1)}, f32[8,40,128]{2,1,0:T(8,128)S(1)}, u32[]{:S(2)}, u32[]{:S(2)}) %collective-permute-start.6) | collective-permute-done | bytes 163872 | tf_op jit(solution)/shard_map/ppermute | solution.py:245
  37.1 0.0 copy-done.6
  37.1 0.0 copy-done
  37.1 0.0 copy-done.1
  37.1 0.0 copy-done.2
  37.1 0.0 copy-done.3
  37.1 0.0 copy-done.4
  37.2 0.0 copy-start.5
  37.2 0.7 copy-done.5
  37.8 20.1 %shard_map.60 = (f32[4096,128]{1,0:T(8,128)}, f32[256,256]{1,0:T(8,128)}) custom-call(f32[16,40,128]{2,1,0:T(8,128)} %get-tuple-element.6.refs_0_, f32[2,40,128]{2,1,0:T(8,128)} %copy-done.6, f32[18,40,128]{2,1,0:T(8,128)} %copy-done.1, f32[18,40,128]{2,1,0:T(8,128)} %copy-done, f32[18,40,128]{2,1,0:T(8,128)} %copy-done.3, f32[18,40,128]{2,1,0:T(8,128)} %copy-done.2, ...), custom_call_target="tpu_custom_call" | custom-call | tf_op jit(solution)/shard_map/pallas_call | solution.py:264
  57.9 15.3 %all_to_all.5 = f32[32,8,256]{2,1,0:T(8,128)S(1)} all-to-all(f32[32,8,256]{2,1,0:T(8,128)} %bitcast.10), channel_id=1, replica_groups=mesh['gx'=4,'gy'=4,'gz'=2] {'gx','gy','gz'}, dimensions={0} | all-to-all | bytes 524288 | tf_op jit(solution)/shard_map/all_to_all | solution.py:276
  73.3 0.6 reduce_sum.9
  (5 shorter events, 0.1 us)
Async XLA Ops:
  2.5 5.2 %collective-permute-start = (f32[2,40,128]{2,1,0:T(8,128)}, f32[2,40,128]{2,1,0:T(8,128)S(1)}, u32[]{:S(2)}, u32[]{:S(2)}) collective-permute-start(f32[2,40,128]{2,1,0:T(8,128)} %get-tuple-element.7), channel_id=1, source_target_pairs={{0,1},{1,0},{2,3},{3,2},{4,5},{5,4},{6,7},{7,6},{8,9},{9,8},{10,11... | collective-permute-start | bytes 122888 | tf_op jit(solution)/shard_map/ppermute | solution.py:223
  7.7 29.4 %copy-start.6 = (f32[2,40,128]{2,1,0:T(8,128)}, f32[2,40,128]{2,1,0:T(8,128)S(1)}, u32[]{:S(2)}) copy-start(f32[2,40,128]{2,1,0:T(8,128)S(1)} %collective-permute-done.refs_1_) | copy-start | bytes 122884
  7.7 8.1 %collective-permute-start.2 = (f32[18,40,128]{2,1,0:T(8,128)S(1)}, f32[18,40,128]{2,1,0:T(8,128)S(1)}, u32[]{:S(2)}, u32[]{:S(2)}) collective-permute-start(f32[18,40,128]{2,1,0:T(8,128)S(1)} %constant_dynamic-update-slice_fusion), channel_id=1, source_target_pairs={{0,24},{8,0},{16,8},{24,16},{1,25},{9,1},{17,9},{25,17},{2,26},{10... | collective-permute-start | bytes 1105928 | tf_op jit(solution)/shard_map/ppermute | solution.py:238
  8.0 10.8 %collective-permute-start.1 = (f32[18,40,128]{2,1,0:T(8,128)S(1)}, f32[18,40,128]{2,1,0:T(8,128)S(1)}, u32[]{:S(2)}, u32[]{:S(2)}) collective-permute-start(f32[18,40,128]{2,1,0:T(8,128)S(1)} %constant_dynamic-update-slice_fusion), channel_id=1, source_target_pairs={{0,8},{8,16},{16,24},{24,0},{1,9},{9,17},{17,25},{25,1},{2,10},{10... | collective-permute-start | bytes 1105928 | tf_op jit(solution)/shard_map/ppermute | solution.py:237
  8.2 14.7 %collective-permute-start.4 = (f32[18,40,128]{2,1,0:T(8,128)S(1)}, f32[18,40,128]{2,1,0:T(8,128)S(1)}, u32[]{:S(2)}, u32[]{:S(2)}) collective-permute-start(f32[18,40,128]{2,1,0:T(8,128)S(1)} %constant_dynamic-update-slice_fusion), channel_id=1, source_target_pairs={{0,6},{2,0},{4,2},{6,4},{1,7},{3,1},{5,3},{7,5},{8,14},{10,8},{12,... | collective-permute-start | bytes 1105928 | tf_op jit(solution)/shard_map/ppermute | solution.py:240
  12.3 17.7 %collective-permute-start.3 = (f32[18,40,128]{2,1,0:T(8,128)S(1)}, f32[18,40,128]{2,1,0:T(8,128)S(1)}, u32[]{:S(2)}, u32[]{:S(2)}) collective-permute-start(f32[18,40,128]{2,1,0:T(8,128)S(1)} %constant_dynamic-update-slice_fusion), channel_id=1, source_target_pairs={{0,2},{2,4},{4,6},{6,0},{1,3},{3,5},{5,7},{7,1},{8,10},{10,12},{12... | collective-permute-start | bytes 1105928 | tf_op jit(solution)/shard_map/ppermute | solution.py:239
  15.8 21.4 %copy-start = (f32[18,40,128]{2,1,0:T(8,128)}, f32[18,40,128]{2,1,0:T(8,128)S(1)}, u32[]{:S(2)}) copy-start(f32[18,40,128]{2,1,0:T(8,128)S(1)} %collective-permute-done.2.refs_3_) | copy-start | bytes 1105924
  18.8 18.4 %copy-start.1 = (f32[18,40,128]{2,1,0:T(8,128)}, f32[18,40,128]{2,1,0:T(8,128)S(1)}, u32[]{:S(2)}) copy-start(f32[18,40,128]{2,1,0:T(8,128)S(1)} %collective-permute-done.1.refs_2_) | copy-start | bytes 1105924
  18.8 14.7 %collective-permute-start.5 = (f32[8,40,128]{2,1,0:T(8,128)S(1)}, f32[8,40,128]{2,1,0:T(8,128)S(1)}, u32[]{:S(2)}, u32[]{:S(2)}) collective-permute-start(f32[8,40,128]{2,1,0:T(8,128)S(1)} %bitcast.12), channel_id=1, source_target_pairs={{0,2},{2,4},{4,6},{6,0},{1,3},{3,5},{5,7},{7,1},{8,10},{10,12},{12... | collective-permute-start | bytes 491528 | tf_op jit(solution)/shard_map/ppermute | solution.py:244
  20.8 16.3 %collective-permute-start.6 = (f32[8,40,128]{2,1,0:T(8,128)S(1)}, f32[8,40,128]{2,1,0:T(8,128)S(1)}, u32[]{:S(2)}, u32[]{:S(2)}) collective-permute-start(f32[8,40,128]{2,1,0:T(8,128)S(1)} %bitcast.11), channel_id=1, source_target_pairs={{0,6},{2,0},{4,2},{6,4},{1,7},{3,1},{5,3},{7,5},{8,14},{10,8},{12,... | collective-permute-start | bytes 491528 | tf_op jit(solution)/shard_map/ppermute | solution.py:245
  22.9 14.2 %copy-start.2 = (f32[18,40,128]{2,1,0:T(8,128)}, f32[18,40,128]{2,1,0:T(8,128)S(1)}, u32[]{:S(2)}) copy-start(f32[18,40,128]{2,1,0:T(8,128)S(1)} %collective-permute-done.4.refs_5_) | copy-start | bytes 1105924
  30.0 7.1 %copy-start.3 = (f32[18,40,128]{2,1,0:T(8,128)}, f32[18,40,128]{2,1,0:T(8,128)S(1)}, u32[]{:S(2)}) copy-start(f32[18,40,128]{2,1,0:T(8,128)S(1)} %collective-permute-done.3.refs_4_) | copy-start | bytes 1105924
  33.5 3.6 %copy-start.4 = (f32[8,40,128]{2,1,0:T(8,128)}, f32[8,40,128]{2,1,0:T(8,128)S(1)}, u32[]{:S(2)}) copy-start(f32[8,40,128]{2,1,0:T(8,128)S(1)} %collective-permute-done.5.refs_6_) | copy-start | bytes 491524
  37.2 0.7 copy-start.5
